TPU v7x, 256 devices: a whole 4x4x8 slice. The times are simulated.
256 devices in a mesh: grp: 8 (over z), dev: 32 (over x, y, core).
Axes of the slice: x: 4, y: 4, z: 8, core: 2. Of those that a mesh axis runs over, the one named last changes fastest.
Arguments:
- blocks: bfloat16 [32768, 128, 128], P(('grp', 'dev')), may hold values from -0.29882812 to 0.29882812
- ids_one: int32 [2, 32768], P(None, ('grp', 'dev')), may hold values from 0 to 2047, as said below
- ids_two: int32 [2, 16384], P(None, ('grp', 'dev')), may hold values from 0 to 1023, as said below
- ids_three: int32 [2, 8192], P(None, ('grp', 'dev')), may hold values from 0 to 511
- match_one: int32 [2048, 128], replicated, may hold values from 0 to 127, as said below
- match_two: int32 [1024, 128], replicated, may hold values from 0 to 127, as said below
- match_three: int32 [512, 128], replicated, may hold values from 0 to 127, as said below
- target_one: int32 [32768], P(('grp', 'dev')), may hold values from 0 to 63
- target_two: int32 [16384], P(('grp', 'dev')), may hold values from 0 to 31
- target_three: int32 [8192], P(('grp', 'dev')), may hold values from 0 to 15
- vertex_weights: float32 [2048, 128], P(('grp', 'dev')), may hold values from 0.1 to 120, as said below
Outputs:
- coarse_graph: float32 [4096, 128, 128], P(('grp', 'dev'))
- rel_weight: float32 [256, 128], P(('grp', 'dev'))
Inputs may be any that keep to these rules, and one draw needn't show every extreme that they name: `match_one`: rows 2b and 2b + 1 together name every number 0 to 127 exactly twice. `match_two`: rows 2b and 2b + 1 together name every number 0 to 127 exactly twice. `match_three`: rows 2b and 2b + 1 together name every number 0 to 127 exactly twice. `ids_one`: a fine block's row and column vertex blocks, halved by integer division, are the ids_two of the coarse slot it goes to. `ids_two`: a first-level block's row and column vertex blocks, halved by integer division, are the ids_three of the coarse slot it goes to. `vertex_weights`: positive.
All inputs are finite; a program needn't handle non-finite values.
Results may differ from a plain program's by a relative error of at most 0.0003.
Values may be sent and summed in bfloat16 or wider, within the bound.
A program may use at most 128 MiB of HBM per device.

v0:
```python
import functools
import math

import jax
import jax.numpy as jnp
from jax import lax
from jax.sharding import Mesh
from jax.sharding import PartitionSpec as P

DEV = ("dev_0", "dev_1", "dev_2")
GRP_DEV = ("grp", "dev_0", "dev_1", "dev_2")


def over_axes(value, axes):
    return functools.reduce(lax.psum, axes, value)


def project(blocks, pair_ids, table):
    row_map = table[pair_ids[0]]
    col_map = table[pair_ids[1]]
    count = blocks.shape[0]
    width = blocks.shape[1]
    group = math.gcd(count, 32)
    lanes = jnp.arange(width, dtype=jnp.int32)
    narrow = blocks.dtype == jnp.bfloat16

    def single(piece):
        block_part, rows_part, cols_part = piece
        right_hot = (cols_part[:, :, None] == lanes).astype(jnp.float32)
        if narrow:
            left_hot = (rows_part[:, :, None] == lanes).astype(jnp.bfloat16)
            halfway = jnp.einsum(
                "gim,gij->gmj", left_hot, block_part, preferred_element_type=jnp.float32
            )
        else:
            left_hot = (rows_part[:, :, None] == lanes).astype(jnp.float32)
            halfway = jnp.einsum(
                "gim,gij->gmj",
                left_hot,
                block_part,
                preferred_element_type=jnp.float32,
                precision=lax.Precision.HIGHEST,
            )
        return jnp.einsum(
            "gmj,gjn->gmn",
            halfway,
            right_hot,
            preferred_element_type=jnp.float32,
            precision=lax.Precision.HIGHEST,
        )

    pieces = (
        blocks.reshape(count // group, group, width, width),
        row_map.reshape(count // group, group, width),
        col_map.reshape(count // group, group, width),
    )
    return lax.map(single, pieces).reshape(count, width, width)


def gather_sum(received, targets, count):
    width = received.shape[1]
    hot = (jnp.arange(count, dtype=jnp.int32)[:, None] == targets[None, :]).astype(jnp.float32)
    flat = jnp.dot(
        hot,
        received.reshape(received.shape[0], width * width),
        preferred_element_type=jnp.float32,
        precision=lax.Precision.HIGHEST,
    )
    return flat.reshape(count, width, width)


def pair_weights(weights, table_rows):
    count, width = weights.shape
    lanes = jnp.arange(width, dtype=jnp.int32)
    hot = (table_rows.reshape(count // 2, 2 * width)[:, :, None] == lanes).astype(jnp.float32)
    return jnp.einsum(
        "kj,kjm->km",
        weights.reshape(count // 2, 2 * width),
        hot,
        preferred_element_type=jnp.float32,
        precision=lax.Precision.HIGHEST,
    )


def per_device(
    blocks,
    ids_one,
    ids_two,
    ids_three,
    match_one,
    match_two,
    match_three,
    target_one,
    target_two,
    target_three,
    vertex_weights,
):
    slots_zero = blocks.shape[0]
    labels = jnp.stack([ids_one[0], ids_one[1], target_one], axis=1)
    fine_in, labels_in = (
        lax.all_to_all(blocks, DEV, split_axis=0, concat_axis=0, tiled=True),
        lax.all_to_all(labels, DEV, split_axis=0, concat_axis=0, tiled=True),
    )
    received = project(fine_in, labels_in[:, :2].T, match_one)
    arrived = labels_in[:, 2]
    coarse_one = gather_sum(received, arrived, slots_zero // 2)
    parts_two = project(coarse_one, ids_two, match_two)
    received_two, arrived_two = (
        lax.all_to_all(parts_two, DEV, split_axis=0, concat_axis=0, tiled=True),
        lax.all_to_all(target_two, DEV, split_axis=0, concat_axis=0, tiled=True),
    )
    coarse_two = gather_sum(received_two, arrived_two, slots_zero // 4)
    parts_three = project(coarse_two, ids_three, match_three)
    received_three, arrived_three = (
        lax.all_to_all(parts_three, "grp", split_axis=0, concat_axis=0, tiled=True),
        lax.all_to_all(target_three, "grp", split_axis=0, concat_axis=0, tiled=True),
    )
    coarse_graph = gather_sum(received_three, arrived_three, slots_zero // 8)
    total = over_axes(jnp.sum(vertex_weights), GRP_DEV)
    owned = vertex_weights.shape[0]
    position = lax.axis_index(GRP_DEV)
    rows_one = lax.dynamic_slice_in_dim(match_one, position * owned, owned, 0)
    weights_one = pair_weights(vertex_weights, rows_one)
    rows_two = lax.dynamic_slice_in_dim(match_two, position * (owned // 2), owned // 2, 0)
    weights_two = pair_weights(weights_one, rows_two)
    rows_three = lax.dynamic_slice_in_dim(match_three, position * (owned // 4), owned // 4, 0)
    weights_three = pair_weights(weights_two, rows_three)
    vertices = weights_three.shape[0] * lax.axis_size(GRP_DEV) * weights_three.shape[1]
    rel_weight = weights_three * vertices / total
    return (coarse_graph, rel_weight)


def solution(mesh):
    finer = Mesh(
        mesh.devices.reshape(mesh.shape["grp"], 4, 4, 2), ("grp", "dev_0", "dev_1", "dev_2")
    )
    in_specs = (
        P(GRP_DEV, None, None),
        P(None, GRP_DEV),
        P(None, GRP_DEV),
        P(None, GRP_DEV),
        P(),
        P(),
        P(),
        P(GRP_DEV),
        P(GRP_DEV),
        P(GRP_DEV),
        P(GRP_DEV, None),
    )
    out_specs = (P(GRP_DEV, None, None), P(GRP_DEV, None))
    return jax.shard_map(
        per_device, mesh=finer, in_specs=in_specs, out_specs=out_specs, check_vma=False
    )
```

profile of v0, /device:TPU:1, one launch (start us, length us, event | category | flops | bytes accessed | tf_op | source)
XLA Modules:
  0.0 327.5 jit_solution(16314661502649924440)
XLA Ops:
  2.5 15.7 %all_to_all.42 = s32[32,4,3]{1,2,0:T(4,128)S(1)} all-to-all(s32[32,4,3]{1,2,0:T(4,128)S(1)} %copy.53), channel_id=1, replica_groups=mesh['grp'=8,'dev_0'=4,'dev_1'=4,'dev_2'=2] {'dev_0','dev_1','dev_2'}, dimensions={0} | all-to-all | bytes 3072 | tf_op jit(solution)/shard_map/all_to_all | solution.py:102
  18.2 5.0 %all-to-all-start.3 = ((bf16[128,128,128]{2,1,0:T(8,128)(2,1)}), bf16[128,128,128]{2,1,0:T(8,128)(2,1)}, u32[]{:S(2)}, u32[]{:S(2)}) async-start(bf16[128,128,128]{2,1,0:T(8,128)(2,1)} %param.15), calls=%async_computation.3 | async-start | bytes 8388608 | tf_op jit(solution)/shard_map/all_to_all | solution.py:101
  26.6 48.8 %all-to-all-done.3 = bf16[128,128,128]{2,1,0:T(8,128)(2,1)} async-done(((bf16[128,128,128]{2,1,0:T(8,128)(2,1)}), bf16[128,128,128]{2,1,0:T(8,128)(2,1)}, u32[]{:S(2)}, u32[]{:S(2)}) %all-to-all-start.3) | async-done | bytes 4194336 | tf_op jit(solution)/shard_map/all_to_all | solution.py:101
  75.4 7.0 %all-to-all-start.1 = ((s32[32,2,1]{1,2,0:T(1,128)}), s32[32,2,1]{1,2,0:T(1,128)S(1)}, u32[]{:S(2)}, u32[]{:S(2)}) async-start(s32[32,2,1]{1,2,0:T(1,128)} %bitcast.4), calls=%async_computation.1 | async-start | bytes 32768 | tf_op jit(solution)/shard_map/all_to_all | solution.py:110
  82.5 20.9 %while.28 = (s32[]{:T(128)}, f32[4,32,128,128]{3,2,1,0:T(8,128)}, s32[4,32,128]{2,1,0:T(8,128)S(1)}, bf16[4,32,128,128]{3,2,1,0:T(8,128)(2,1)}, s32[4,32,128]{2,1,0:T(8,128)S(1)}, /*index=5*/s32[]{:T(128)}) while((s32[]{:T(128)}, f32[4,32,128,128]{3,2,1,0:T(8,128)}, s32[4,32,128]{2,1,0:T(8,128)S(1)}, ...), condition=%wide.region_1.2_spmd.clone.clone, body=%wide.region_0.1_spmd.clone.clone.sunk | while | flops 940572672 | bytes 7439433 | solution.py:57
  82.5 2.6 fusion.66
  85.1 2.7 bitcast_dynamic-update-slice_fusion.4
  87.7 2.6 fusion.66
  90.3 2.6 bitcast_dynamic-update-slice_fusion.4
  92.9 2.6 fusion.66
  95.5 2.7 bitcast_dynamic-update-slice_fusion.4
  98.2 2.6 fusion.66
  100.7 2.6 bitcast_dynamic-update-slice_fusion.4
  103.4 13.1 %copy.93 = f32[16,8,128,128]{3,1,2,0:T(8,128)} copy(f32[16,8,128,128]{3,2,1,0:T(8,128)} %bitcast.158) | data formatting | bytes 16777216
  116.5 9.0 %copy.55 = f32[16384,128]{1,0:T(8,128)} copy(f32[16384,128]{0,1:T(8,128)} %bitcast.157) | data formatting | bytes 16777216 | tf_op jit(solution)/shard_map/dot_general | solution.py:63
  125.5 10.3 %fusion.35 = f32[2,32,128,128]{3,1,2,0:T(8,128)} fusion(f32[128,128,128,1]{2,1,0,3:T(8,128)} %bitcast.156, s32[128]{0:T(128)S(1)} %slice_bitcast_fusion.1, s32[2,32]{1,0:T(2,128)S(1)} %multiply_add_fusion), kind=kOutput, calls=%fused_computation.61 | convolution fusion | flops 1610620928 | bytes 12583680 | tf_op jit(solution)/shard_map/dot_general | solution.py:63
  135.9 17.3 %while.29 = (s32[]{:T(128)}, f32[2,32,128,128]{3,2,1,0:T(8,128)}, s32[2,32,128]{2,1,0:T(8,128)S(1)}, f32[2,32,128,128]{3,1,2,0:T(8,128)}, s32[2,32,128]{2,1,0:T(8,128)S(1)}, /*index=5*/s32[]{:T(128)}) while((s32[]{:T(128)}, f32[2,32,128,128]{3,2,1,0:T(8,128)}, s32[2,32,128]{2,1,0:T(8,128)S(1)}, ...), condition=%wide.region_3.4_spmd.clone.clone, body=%wide.region_2.3_spmd.clone.clone.sunk | while | flops 1611661312 | bytes 12681805 | solution.py:57
  137.6 4.2 %fusion.68 = f32[32,128,128]{2,1,0:T(8,128)S(1)} fusion(f32[1,32,128,128]{3,1,2,0:T(8,128)S(1)} %constant_dynamic-slice_fusion.4, s32[32,128]{1,0:T(8,128)S(1)} %get-tuple-element.287), kind=kOutput, calls=%fused_computation.23.clone.1 | convolution fusion | flops 805830656 | bytes 4210688 | tf_op jit(solution)/shard_map/while/body/eval_jaxpr/gim,gij->gmj/dot_general | solution.py:37
  141.9 2.7 bitcast_dynamic-update-slice_fusion.5
  146.3 4.2 %fusion.68 = f32[32,128,128]{2,1,0:T(8,128)S(1)} fusion(f32[1,32,128,128]{3,1,2,0:T(8,128)S(1)} %constant_dynamic-slice_fusion.4, s32[32,128]{1,0:T(8,128)S(1)} %get-tuple-element.287), kind=kOutput, calls=%fused_computation.23.clone.1 | convolution fusion | flops 805830656 | bytes 4210688 | tf_op jit(solution)/shard_map/while/body/eval_jaxpr/gim,gij->gmj/dot_general | solution.py:37
  150.5 2.6 bitcast_dynamic-update-slice_fusion.5
  153.2 7.6 %all-to-all-start.4 = ((f32[64,128,128]{2,1,0:T(8,128)}), f32[64,128,128]{2,1,0:T(8,128)}, u32[]{:S(2)}, u32[]{:S(2)}) async-start(f32[64,128,128]{2,1,0:T(8,128)} %bitcast.26), calls=%async_computation.4 | async-start | bytes 8388608 | tf_op jit(solution)/shard_map/all_to_all | solution.py:109
  164.1 48.8 %all-to-all-done.4 = f32[64,128,128]{2,1,0:T(8,128)} async-done(((f32[64,128,128]{2,1,0:T(8,128)}), f32[64,128,128]{2,1,0:T(8,128)}, u32[]{:S(2)}, u32[]{:S(2)}) %all-to-all-start.4) | async-done | bytes 4194336 | tf_op jit(solution)/shard_map/all_to_all | solution.py:109
  212.9 8.2 %all-to-all-start = ((s32[8,4,1]{1,2,0:T(1,128)}), s32[8,4,1]{1,2,0:T(1,128)S(1)}, u32[]{:S(2)}, u32[]{:S(2)}) async-start(s32[8,4,1]{1,2,0:T(1,128)} %bitcast), calls=%async_computation | async-start | bytes 8192 | tf_op jit(solution)/shard_map/all_to_all | solution.py:116
  221.1 6.1 %fusion.15 = f32[32,128,128]{2,0,1:T(8,128)S(1)} fusion(s32[64]{0:T(128)S(1)} %eq.224, f32[8,8,128,128]{3,2,1,0:T(8,128)} %bitcast.64), kind=kOutput, calls=%fused_computation.33 | convolution fusion | flops 402655232 | bytes 6291712 | tf_op jit(solution)/shard_map/dot_general | solution.py:63
  227.2 2.6 fusion.21
  229.8 2.7 fusion.23
  232.5 6.8 %all-to-all-start.5 = ((f32[32,128,128]{2,1,0:T(8,128)}), f32[32,128,128]{2,1,0:T(8,128)S(1)}, u32[]{:S(2)}, u32[]{:S(2)}) async-start(f32[32,128,128]{2,1,0:T(8,128)} %fusion.23), calls=%async_computation.5 | async-start | bytes 4194304 | tf_op jit(solution)/shard_map/all_to_all | solution.py:115
  239.8 55.5 %psum.28 = f32[]{:T(128)} all-reduce(f32[]{:T(128)} %reduce_sum.9), channel_id=1, replica_groups=mesh['grp'=8,'dev_0'=4,'dev_1'=4,'dev_2'=2] {'grp'}, use_global_device_ids=true, to_apply=%region_5.6 | all-reduce | flops 1 | bytes 8 | tf_op jit(solution)/shard_map/psum | solution.py:15
  295.4 7.3 %psum.29 = f32[]{:T(128)} all-reduce(f32[]{:T(128)} %psum.28), channel_id=1, replica_groups=mesh['grp'=8,'dev_0'=4,'dev_1'=4,'dev_2'=2] {'dev_0'}, use_global_device_ids=true, to_apply=%region_6.7 | all-reduce | flops 1 | bytes 8 | tf_op jit(solution)/shard_map/psum | solution.py:15
  302.6 8.3 %psum.30 = f32[]{:T(128)} all-reduce(f32[]{:T(128)} %psum.29), channel_id=1, replica_groups=mesh['grp'=8,'dev_0'=4,'dev_1'=4,'dev_2'=2] {'dev_1'}, use_global_device_ids=true, to_apply=%region_7.8 | all-reduce | flops 1 | bytes 8 | tf_op jit(solution)/shard_map/psum | solution.py:15
  311.0 9.7 %psum.31 = f32[]{:T(128)} all-reduce(f32[]{:T(128)} %psum.30), channel_id=1, replica_groups=mesh['grp'=8,'dev_0'=4,'dev_1'=4,'dev_2'=2] {'dev_2'}, use_global_device_ids=true, to_apply=%region_8.9 | all-reduce | flops 1 | bytes 8 | tf_op jit(solution)/shard_map/psum | solution.py:15
  (71 shorter events, 19.5 us)
Async XLA Ops:
  0.6 24.7 %copy-start = (s32[2048,128]{1,0:T(8,128)S(1)}, s32[2048,128]{1,0:T(8,128)}, u32[]{:S(2)}) copy-start(s32[2048,128]{1,0:T(8,128)} %param.19) | copy-start | bytes 3145732
  18.2 5.0 %copy-start.4 = (s32[2,64]{1,0:T(2,128)S(1)}, s32[2,64]{1,0:T(2,128)}, u32[]{:S(2)}) copy-start(s32[2,64]{1,0:T(2,128)} %param.17) | copy-start | bytes 1540
  18.2 5.0 %copy-start.1 = (s32[1024,128]{1,0:T(8,128)S(1)}, s32[1024,128]{1,0:T(8,128)}, u32[]{:S(2)}) copy-start(s32[1024,128]{1,0:T(8,128)} %param.20) | copy-start | bytes 1572868
  18.2 6.2 %copy-start.6 = (s32[64]{0:T(128)S(1)}, s32[64]{0:T(128)}, u32[]{:S(2)}) copy-start(s32[64]{0:T(128)} %param.23) | copy-start | bytes 772
  18.2 57.2 %all-to-all-start.3 = ((bf16[128,128,128]{2,1,0:T(8,128)(2,1)}), bf16[128,128,128]{2,1,0:T(8,128)(2,1)}, u32[]{:S(2)}, u32[]{:S(2)}) async-start(bf16[128,128,128]{2,1,0:T(8,128)(2,1)} %param.15), calls=%async_computation.3 | async-start | bytes 8388608 | tf_op jit(solution)/shard_map/all_to_all | solution.py:101
  75.4 77.8 %all-to-all-start.1 = ((s32[32,2,1]{1,2,0:T(1,128)}), s32[32,2,1]{1,2,0:T(1,128)S(1)}, u32[]{:S(2)}, u32[]{:S(2)}) async-start(s32[32,2,1]{1,2,0:T(1,128)} %bitcast.4), calls=%async_computation.1 | async-start | bytes 32768 | tf_op jit(solution)/shard_map/all_to_all | solution.py:110
  153.2 7.6 %copy-start.5 = (s32[2,32]{1,0:T(2,128)S(1)}, s32[2,32]{1,0:T(2,128)}, u32[]{:S(2)}) copy-start(s32[2,32]{1,0:T(2,128)} %param.18) | copy-start | bytes 772
  153.2 7.6 %copy-start.2 = (s32[512,128]{1,0:T(8,128)S(1)}, s32[512,128]{1,0:T(8,128)}, u32[]{:S(2)}) copy-start(s32[512,128]{1,0:T(8,128)} %param.21) | copy-start | bytes 786436
  153.2 8.8 %copy-start.7 = (s32[32]{0:T(128)S(1)}, s32[32]{0:T(128)}, u32[]{:S(2)}) copy-start(s32[32]{0:T(128)} %param.24) | copy-start | bytes 388
  153.2 59.7 %all-to-all-start.4 = ((f32[64,128,128]{2,1,0:T(8,128)}), f32[64,128,128]{2,1,0:T(8,128)}, u32[]{:S(2)}, u32[]{:S(2)}) async-start(f32[64,128,128]{2,1,0:T(8,128)} %bitcast.26), calls=%async_computation.4 | async-start | bytes 8388608 | tf_op jit(solution)/shard_map/all_to_all | solution.py:109
  212.9 19.6 %all-to-all-start = ((s32[8,4,1]{1,2,0:T(1,128)}), s32[8,4,1]{1,2,0:T(1,128)S(1)}, u32[]{:S(2)}, u32[]{:S(2)}) async-start(s32[8,4,1]{1,2,0:T(1,128)} %bitcast), calls=%async_computation | async-start | bytes 8192 | tf_op jit(solution)/shard_map/all_to_all | solution.py:116
  232.5 6.8 %copy-start.3 = (f32[8,128]{1,0:T(8,128)S(1)}, f32[8,128]{1,0:T(8,128)}, u32[]{:S(2)}) copy-start(f32[8,128]{1,0:T(8,128)} %param.25) | copy-start | bytes 12292
  232.5 91.8 %all-to-all-start.5 = ((f32[32,128,128]{2,1,0:T(8,128)}), f32[32,128,128]{2,1,0:T(8,128)S(1)}, u32[]{:S(2)}, u32[]{:S(2)}) async-start(f32[32,128,128]{2,1,0:T(8,128)} %fusion.23), calls=%async_computation.5 | async-start | bytes 4194304 | tf_op jit(solution)/shard_map/all_to_all | solution.py:115
where the time goes:
time: 329 us; the launch traced here: 328 us
  waiting for transfers between devices  97.6 us (30%)
  blocking collectives  96.5 us (29%)
  matrix products  60.4 us (18%)
  local copies, waits for them, and re-layouts  35.4 us (11%)
  starting transfers between devices  34.6 us (11%)
    psum x4, blocking collectives, over_axes(): return functools.reduce(lax.psum, axes, value)  80.8 us
    all_to_all x1, waiting for transfers between devices, per_device(): lax.all_to_all(parts_two, DEV, split_axis=0, concat_axis=0, tiled=True)  48.8 us
    all_to_all x1, waiting for transfers between devices, per_device(): lax.all_to_all(blocks, DEV, split_axis=0, concat_axis=0, tiled=True)  48.8 us
    dot_general x7, matrix products, single(): jnp.einsum('gim,gij->gmj', left_hot, block_part, preferred_element_type=j...  21.3 us
    dot_general x7, matrix products, single(): jnp.einsum('gmj,gjn->gmn', halfway, right_hot, preferred_element_type=jnp...  18.6 us
    dot_general x3, matrix products, gather_sum(): jnp.dot(hot, received.reshape(received.shape[0], width * width), preferre...  18.4 us
    all_to_all x1, blocking collectives, per_device(): lax.all_to_all(labels, DEV, split_axis=0, concat_axis=0, tiled=True)  15.7 us
    unnamed x18, local copies, waits for them, and re-layouts  14.5 us
  transfers between devices with their start and end apart: 5, of which 2 were waited for; matrix products, arithmetic and copies ran while one was open for 28% of the time, Pallas kernels for 0%

commit v1 on v0

v1 whole, which is shorter than its diff:
```python
import functools

import jax
import jax.numpy as jnp
from jax import lax
from jax.experimental import pallas as pl
from jax.experimental.pallas import tpu as pltpu
from jax.sharding import PartitionSpec as P

MESH = pl.DeviceIdType.MESH
BLOCK = 128
PITCH = 136
CHUNKS = 2
ROWS = BLOCK // CHUNKS
SPAN = ROWS + 8
TOP = 32767.0
TINY = 1e-30
ROUNDS = (
    ((0, 0),),
    ((0, 1), (1, 1), (0, 3), (3, 3)),
    ((1, 0), (1, 3), (3, 0), (3, 1)),
    ((0, 2), (2, 1), (2, 3)),
    ((2, 0), (1, 2), (3, 2)),
    ((2, 2),),
)
ORDER = tuple(
    (dx, dy, dc) for turn in ROUNDS for dc in (0, 1) for dx, dy in turn if (dx, dy, dc) != (0, 0, 0)
)
RING = (1, 7, 2, 6, 3, 5, 4)


def dest_of(v, dx, dy, dc):
    x, y, c = v // 8, lax.rem(v // 2, 4), lax.rem(v, 2)
    ddx = jnp.where(c == 1, dy, dx)
    ddy = jnp.where(c == 1, dx, dy)
    return lax.rem(x + ddx, 4) * 8 + lax.rem(y + ddy, 4) * 2 + lax.rem(c + dc, 2)


def source_of(v, turn):
    code = jnp.int32(0)
    for place, (dx, dy, dc) in enumerate(ORDER):
        code = jnp.where(turn == place + 1, dx * 8 + dy * 2 + dc, code)
    dx, dy, dc = code // 8, lax.rem(code // 2, 4), lax.rem(code, 2)
    x, y, c = v // 8, lax.rem(v // 2, 4), lax.rem(v, 2)
    other = lax.rem(c + dc, 2)
    ddx = jnp.where(other == 1, dy, dx)
    ddy = jnp.where(other == 1, dx, dy)
    return lax.rem(x + 4 - ddx, 4) * 8 + lax.rem(y + 4 - ddy, 4) * 2 + other


def split(value):
    high = value.astype(jnp.bfloat16)
    return high, (value - high.astype(jnp.float32)).astype(jnp.bfloat16)


def one_hot(lanes, count):
    width = lanes.shape[1]
    rows = lax.broadcasted_iota(jnp.int32, (count, width), 0).astype(jnp.float32)
    return jnp.where(rows == lanes, 1.0, 0.0).astype(jnp.bfloat16)


def send(src, dst, send_sem, recv_sem, device):
    pltpu.make_async_remote_copy(
        src_ref=src, dst_ref=dst, send_sem=send_sem, recv_sem=recv_sem, device_id=device, device_id_type=MESH
    ).start()


def wait(ref, sem):
    pltpu.make_async_copy(ref, ref, sem).wait()


def kernel(
    blocks, ids, one, two, three, target_one, target_two, target_three, weights,
    graph, relative,
    fine, maps_out, maps_in, tags_out, tags_in, zags_out, zags_in, projected, coarse_one, out_two, in_two,
    size_two, sizein_two, spread, coarse_two, out_three, in_three, size_three, sizein_three, weighted,
    fine_send, fine_recv, maps_sem, tags_sem, zags_sem, two_sem, sizetwo_sem, three_sem, sizethree_sem,
):
    g, v = lax.axis_index("grp"), lax.axis_index("dev")
    barrier = pltpu.get_barrier_semaphore()
    for step in ORDER:
        pl.semaphore_signal(barrier, inc=1, device_id=(g, dest_of(v, *step)), device_id_type=MESH)
    for step in RING:
        pl.semaphore_signal(barrier, inc=1, device_id=(lax.rem(g + step, 8), v), device_id_type=MESH)
    mine = pltpu.make_async_copy(blocks.at[pl.ds(v * 4, 4)], fine.at[pl.ds(v * 4, 4)], fine_recv.at[v])
    mine.start()

    def composed(numbers):
        first = jnp.concatenate([one[pl.ds(n, 1), :] for n in numbers], axis=0)
        second = jnp.concatenate([two[pl.ds(n // 2, 1), :] for n in numbers], axis=0)
        third = jnp.concatenate([three[pl.ds(n // 4, 1), :] for n in numbers], axis=0)
        second = jnp.take_along_axis(second, first, axis=1)
        return jnp.take_along_axis(third, second, axis=1).astype(jnp.float32)

    def make_maps(w, carry):
        numbers = [ids[a, w * 4 + j] for a in range(2) for j in range(4)]
        maps_out[w] = composed(numbers).astype(jnp.bfloat16)
        return carry

    lax.fori_loop(0, 32, make_maps, 0)
    maps_in[v] = maps_out[v]

    lane = lax.broadcasted_iota(jnp.int32, (32, BLOCK), 1)
    row = lax.broadcasted_iota(jnp.int32, (32, BLOCK), 0)
    local = weights[...]
    partial = jnp.sum(jnp.sum(local, axis=0, keepdims=True), axis=1, keepdims=True)

    def spread_tags(table, per, count, place):
        index = lax.rem(count * 0 + row * per + lax.rem(lane, per), BLOCK)
        picked = jnp.take_along_axis(jnp.broadcast_to(table, (32, BLOCK)), index, axis=1)
        return jnp.where(lane // per == place, picked, 0).astype(jnp.float32)

    tags_one = spread_tags(target_one[...], 4, 32, v)
    tags_two = spread_tags(target_two[...], 2, 32, v)
    tags_two = tags_two + jnp.where(lane == v + 64, partial, 0.0)
    for w in range(32):
        tags_out[w, 0:1, :] = tags_one[w : w + 1]
        tags_out[w, 1:2, :] = tags_two[w : w + 1]
    tags_in[v] = tags_out[v]

    pl.semaphore_wait(barrier, len(ORDER) + len(RING))
    for step in ORDER:
        w = dest_of(v, *step)
        send(maps_out.at[w], maps_in.at[v], maps_sem.at[0], maps_sem.at[1], (g, w))
        send(tags_out.at[w], tags_in.at[v], tags_sem.at[0], tags_sem.at[1], (g, w))
    for place, step in enumerate(ORDER):
        w = dest_of(v, *step)
        send(
            blocks.at[pl.ds(w * 4, 4)], fine.at[pl.ds(v * 4, 4)], fine_send.at[place], fine_recv.at[v], (g, w)
        )

    base = (g * 32 + v) * 8
    own = composed([base + e for e in range(8)])
    part = lax.broadcasted_iota(jnp.int32, (8, BLOCK), 0)
    total_here = jnp.zeros((8, BLOCK), jnp.float32)
    up = lax.broadcasted_iota(jnp.int32, (BLOCK, BLOCK), 0).astype(jnp.float32)
    for e in range(8):
        hot = jnp.where(up == own[e : e + 1], 1.0, 0.0)
        total_here = total_here + lax.dot_general(
            jnp.where(part == e, local, 0.0), hot, (((1,), (1,)), ((), ())),
            precision=lax.Precision.HIGHEST, preferred_element_type=jnp.float32,
        )
    weighted[...] = jnp.sum(total_here, axis=0, keepdims=True)

    wait(maps_in.at[pl.ds(0, 31)], maps_sem.at[1])
    wait(tags_in.at[pl.ds(0, 31)], tags_sem.at[1])

    def project(turn, carry):
        s = source_of(v, turn)
        wait(fine.at[pl.ds(s * 4, 4)], fine_recv.at[s])
        maps = maps_in[s].astype(jnp.float32)
        for j in range(4):
            left = one_hot(maps[j : j + 1], BLOCK)
            right = one_hot(maps[4 + j : 5 + j], BLOCK)
            halfway = jnp.dot(left, fine[s * 4 + j], preferred_element_type=jnp.float32)
            both = jnp.concatenate(split(halfway), axis=0)
            full = lax.dot_general(
                both, right, (((1,), (1,)), ((), ())), preferred_element_type=jnp.float32
            )
            start = pl.multiple_of((s * 4 + j) * PITCH, 8)
            projected[pl.ds(start, BLOCK), :] = full[:BLOCK] + full[BLOCK:]
        return carry

    lax.fori_loop(0, 32, project, 0)

    tags = jnp.sum(tags_in[...], axis=0)
    hot_one = one_hot(tags[0:1], 64)
    hot_one = jnp.concatenate([hot_one, hot_one], axis=1)
    hot_two = one_hot(tags[1:2], 32)[:, :64]
    hot_two = jnp.concatenate([hot_two, hot_two], axis=1)
    beyond = lax.broadcasted_iota(jnp.int32, (1, BLOCK), 1)
    group_total = jnp.sum(jnp.where(beyond >= 64, tags[1:2], 0.0), axis=1, keepdims=True)

    lane8 = lax.broadcasted_iota(jnp.int32, (8, BLOCK), 1)
    row8 = lax.broadcasted_iota(jnp.int32, (8, BLOCK), 0)
    picked = jnp.take_along_axis(
        jnp.broadcast_to(target_three[...], (8, BLOCK)), row8 * 4 + lax.rem(lane8, 4), axis=1
    )
    tags_three = jnp.where(lane8 // 4 == g, picked, 0).astype(jnp.float32)
    totals = jnp.where(beyond == g, group_total, 0.0)
    for h in range(8):
        zags_out[h, 0:1, :] = tags_three[h : h + 1]
        zags_out[h, 1:2, :] = totals
    zags_in[g] = zags_out[g]
    for step in RING:
        h = lax.rem(g + step, 8)
        send(zags_out.at[h], zags_in.at[g], zags_sem.at[0], zags_sem.at[1], (h, v))

    def quantize(source, count, chunk, out, size, per):
        def one_block(s, carry):
            value = source[pl.ds(pl.multiple_of(s * PITCH + chunk * ROWS, 8), ROWS), :]
            top = jnp.max(jnp.abs(value), axis=0, keepdims=True)
            top = jnp.maximum(top, TINY)
            scaled = jnp.round(value * (TOP / top))
            out[chunk, s] = scaled.astype(jnp.int32).astype(jnp.int16)
            size[chunk, s] = top
            return carry

        lax.fori_loop(0, count, one_block, 0, unroll=4)

    def restore(source, size, count, chunk):
        def one_block(s, carry):
            value = source[chunk, s].astype(jnp.int32).astype(jnp.float32)
            spread[pl.ds(pl.multiple_of(s * SPAN, 8), ROWS), :] = value * (size[chunk, s] * (1.0 / TOP))
            return carry

        lax.fori_loop(0, count, one_block, 0, unroll=4)

    def add_up(source, pitch, count, first, hot, store):
        def one_row(m, carry):
            value = source[pl.ds(first + m, count, stride=pitch), :]
            both = jnp.concatenate(split(value), axis=0)
            store(m, jnp.dot(hot, both, preferred_element_type=jnp.float32))
            return carry

        lax.fori_loop(0, ROWS, one_row, 0, unroll=8)

    for chunk in range(CHUNKS):

        def keep_one(m, value, chunk=chunk):
            coarse_one[pl.ds(chunk * ROWS + m, 64, stride=PITCH), :] = value

        add_up(projected, PITCH, BLOCK, chunk * ROWS, hot_one, keep_one)
        quantize(coarse_one, 64, chunk, out_two, size_two, 2)
        here = pl.ds(v * 2, 2)
        in_two[chunk, here] = out_two[chunk, here]
        sizein_two[chunk, here] = size_two[chunk, here]
        for step in ORDER:
            w = dest_of(v, *step)
            there = pl.ds(w * 2, 2)
            send(
                size_two.at[chunk, there], sizein_two.at[chunk, here],
                sizetwo_sem.at[0, chunk], sizetwo_sem.at[1, chunk], (g, w),
            )
            send(
                out_two.at[chunk, there], in_two.at[chunk, here],
                two_sem.at[0, chunk], two_sem.at[1, chunk], (g, w),
            )

    wait(zags_in.at[pl.ds(0, 7)], zags_sem.at[1])
    zags = jnp.sum(zags_in[...], axis=0)
    hot_three = one_hot(zags[0:1], 16)[:, :32]
    hot_three = jnp.concatenate([hot_three, hot_three], axis=1)
    relative[...] = weighted[...] * 32768.0 / jnp.sum(zags[1:2], axis=1, keepdims=True)

    for chunk in range(CHUNKS):
        wait(sizein_two.at[chunk, pl.ds(0, 62)], sizetwo_sem.at[1, chunk])
        wait(in_two.at[chunk, pl.ds(0, 62)], two_sem.at[1, chunk])
        restore(in_two, sizein_two, 64, chunk)

        def keep_two(m, value, chunk=chunk):
            coarse_two[pl.ds(chunk * ROWS + m, 32, stride=PITCH), :] = value

        add_up(spread, SPAN, 64, 0, hot_two, keep_two)
        quantize(coarse_two, 32, chunk, out_three, size_three, 4)
        here = pl.ds(g * 4, 4)
        in_three[chunk, here] = out_three[chunk, here]
        sizein_three[chunk, here] = size_three[chunk, here]
        for step in RING:
            h = lax.rem(g + step, 8)
            there = pl.ds(h * 4, 4)
            send(
                size_three.at[chunk, there], sizein_three.at[chunk, here],
                sizethree_sem.at[0, chunk], sizethree_sem.at[1, chunk], (h, v),
            )
            send(
                out_three.at[chunk, there], in_three.at[chunk, here],
                three_sem.at[0, chunk], three_sem.at[1, chunk], (h, v),
            )

    for chunk in range(CHUNKS):
        wait(sizein_three.at[chunk, pl.ds(0, 28)], sizethree_sem.at[1, chunk])
        wait(in_three.at[chunk, pl.ds(0, 28)], three_sem.at[1, chunk])
        restore(in_three, sizein_three, 32, chunk)

        def keep_three(m, value, chunk=chunk):
            graph[pl.ds(chunk * ROWS + m, 16, stride=BLOCK), :] = value

        add_up(spread, SPAN, 32, 0, hot_three, keep_three)

    for place, step in enumerate(ORDER):
        w = dest_of(v, *step)
        wait(blocks.at[pl.ds(w * 4, 4)], fine_send.at[place])
    wait(maps_in.at[pl.ds(0, 31)], maps_sem.at[0])
    wait(tags_in.at[pl.ds(0, 31)], tags_sem.at[0])
    wait(zags_in.at[pl.ds(0, 7)], zags_sem.at[0])
    for chunk in range(CHUNKS):
        wait(size_two.at[chunk, pl.ds(0, 62)], sizetwo_sem.at[0, chunk])
        wait(out_two.at[chunk, pl.ds(0, 62)], two_sem.at[0, chunk])
        wait(size_three.at[chunk, pl.ds(0, 28)], sizethree_sem.at[0, chunk])
        wait(out_three.at[chunk, pl.ds(0, 28)], three_sem.at[0, chunk])


def pad_lanes(values):
    return jnp.pad(values, (0, BLOCK - values.shape[0])).reshape(1, BLOCK)


def per_device(
    blocks, ids_one, ids_two, ids_three, match_one, match_two, match_three,
    target_one, target_two, target_three, vertex_weights,
):
    del ids_two, ids_three
    vmem = pl.BlockSpec(memory_space=pltpu.VMEM)
    f32, i16, bf16 = jnp.float32, jnp.int16, jnp.bfloat16
    graph, relative = pl.pallas_call(
        kernel,
        out_shape=(
            jax.ShapeDtypeStruct((16 * BLOCK, BLOCK), f32),
            jax.ShapeDtypeStruct((1, BLOCK), f32),
        ),
        in_specs=[pl.BlockSpec(memory_space=pl.ANY), pl.BlockSpec(memory_space=pltpu.SMEM)] + [vmem] * 7,
        out_specs=(vmem, vmem),
        scratch_shapes=[
            pltpu.VMEM((128, BLOCK, BLOCK), bf16),
            pltpu.VMEM((32, 8, BLOCK), bf16),
            pltpu.VMEM((32, 8, BLOCK), bf16),
            pltpu.VMEM((32, 2, BLOCK), f32),
            pltpu.VMEM((32, 2, BLOCK), f32),
            pltpu.VMEM((8, 2, BLOCK), f32),
            pltpu.VMEM((8, 2, BLOCK), f32),
            pltpu.VMEM((128 * PITCH, BLOCK), f32),
            pltpu.VMEM((64 * PITCH, BLOCK), f32),
            pltpu.VMEM((CHUNKS, 64, ROWS, BLOCK), i16),
            pltpu.VMEM((CHUNKS, 64, ROWS, BLOCK), i16),
            pltpu.VMEM((CHUNKS, 64, 1, BLOCK), f32),
            pltpu.VMEM((CHUNKS, 64, 1, BLOCK), f32),
            pltpu.VMEM((64 * SPAN, BLOCK), f32),
            pltpu.VMEM((32 * PITCH, BLOCK), f32),
            pltpu.VMEM((CHUNKS, 32, ROWS, BLOCK), i16),
            pltpu.VMEM((CHUNKS, 32, ROWS, BLOCK), i16),
            pltpu.VMEM((CHUNKS, 32, 1, BLOCK), f32),
            pltpu.VMEM((CHUNKS, 32, 1, BLOCK), f32),
            pltpu.VMEM((1, BLOCK), f32),
            pltpu.SemaphoreType.DMA((31,)),
            pltpu.SemaphoreType.DMA((32,)),
            pltpu.SemaphoreType.DMA((2,)),
            pltpu.SemaphoreType.DMA((2,)),
            pltpu.SemaphoreType.DMA((2,)),
            pltpu.SemaphoreType.DMA((2, CHUNKS)),
            pltpu.SemaphoreType.DMA((2, CHUNKS)),
            pltpu.SemaphoreType.DMA((2, CHUNKS)),
            pltpu.SemaphoreType.DMA((2, CHUNKS)),
        ],
        compiler_params=pltpu.CompilerParams(
            collective_id=0, has_side_effects=True, vmem_limit_bytes=56 * 2**20
        ),
        name="coarsen",
    )(
        blocks, ids_one, match_one, match_two, match_three,
        target_one.reshape(1, BLOCK), pad_lanes(target_two), pad_lanes(target_three), vertex_weights,
    )
    return graph.reshape(16, BLOCK, BLOCK), relative


def solution(mesh):
    both = ("grp", "dev")
    in_specs = (
        P(both, None, None), P(None, both), P(None, both), P(None, both), P(), P(), P(),
        P(both), P(both), P(both), P(both, None),
    )
    return jax.shard_map(
        per_device, mesh=mesh, in_specs=in_specs, out_specs=(P(both, None, None), P(both, None)), check_vma=False
    )
```

time: 329 us -> 123 us (0.37)
  the two profiles are of different devices: /device:TPU:1 before, /device:TPU:2 now
where the time goes in v1:
time: 123 us
  Pallas kernels  118 us (96%)
  local copies, waits for them, and re-layouts  4.62 us (4%)
    pallas_call x1, Pallas kernels, per_device(): pl.pallas_call(kernel, out_shape=(jax.ShapeDtypeStruct((16 * BLOCK, BLOCK...  118 us
    unnamed x2, local copies, waits for them, and re-layouts  3.43 us

profile of v1, /device:TPU:2, one launch (start us, length us, event | category | flops | bytes accessed | tf_op | source)
XLA Modules:
  0.0 122.9 jit_solution(2455666847509968340)
XLA Ops:
  0.6 1.2 pad_bitcast_fusion
  1.8 117.6 %coarsen.1 = (f32[2048,128]{1,0:T(8,128)}, f32[1,128]{1,0:T(1,128)}) custom-call(bf16[128,128,128]{2,1,0:T(8,128)(2,1)} %blocks.1, s32[2,128]{1,0:T(2,128)} %ids.1, s32[2048,128]{1,0:T(8,128)} %one.1, s32[1024,128]{1,0:T(8,128)} %two.1, s32[512,128]{1,0:T(8,128)} %three.1, s32[1,128]{1,0:T(1,128)} %bitcast.7, s32[1,128]{1,0:T(1,128)} %get-tuple-element.7.target_two, ...), custom_call_target="tpu_custom_call" | custom-call | tf_op jit(solution)/shard_map/coarsen/pallas_call | solution.py:305
  119.4 2.3 %copy.13 = f32[16,128,128]{2,1,0:T(8,128)} copy(f32[16,128,128]{2,1,0:T(8,128)} %bitcast.6) | data formatting | bytes 2097152
  121.7 1.1 copy.14

commit v2 on v1

v2 whole, which is shorter than its diff:
```python
import functools

import jax
import jax.numpy as jnp
from jax import lax
from jax.experimental import pallas as pl
from jax.experimental.pallas import tpu as pltpu
from jax.sharding import PartitionSpec as P

MESH = pl.DeviceIdType.MESH
BLOCK = 128
PITCH = 136
CHUNKS = 8
AHEAD = 3
FIRST = 5
ROWS = BLOCK // CHUNKS
SPAN = ROWS + 8
TOP = 32767.0
TINY = 1e-30
ROUNDS = (
    ((0, 0),),
    ((0, 1), (1, 1), (0, 3), (3, 3)),
    ((1, 0), (1, 3), (3, 0), (3, 1)),
    ((0, 2), (2, 1), (2, 3)),
    ((2, 0), (1, 2), (3, 2)),
    ((2, 2),),
)
ORDER = tuple(
    (dx, dy, dc) for turn in ROUNDS for dc in (0, 1) for dx, dy in turn if (dx, dy, dc) != (0, 0, 0)
)
RING = (1, 7, 2, 6, 3, 5, 4)


def dest_of(v, dx, dy, dc):
    x, y, c = v // 8, lax.rem(v // 2, 4), lax.rem(v, 2)
    ddx = jnp.where(c == 1, dy, dx)
    ddy = jnp.where(c == 1, dx, dy)
    return lax.rem(x + ddx, 4) * 8 + lax.rem(y + ddy, 4) * 2 + lax.rem(c + dc, 2)


def source_of(v, turn):
    code = jnp.int32(0)
    for place, (dx, dy, dc) in enumerate(ORDER):
        code = jnp.where(turn == place + 1, dx * 8 + dy * 2 + dc, code)
    dx, dy, dc = code // 8, lax.rem(code // 2, 4), lax.rem(code, 2)
    x, y, c = v // 8, lax.rem(v // 2, 4), lax.rem(v, 2)
    other = lax.rem(c + dc, 2)
    ddx = jnp.where(other == 1, dy, dx)
    ddy = jnp.where(other == 1, dx, dy)
    return lax.rem(x + 4 - ddx, 4) * 8 + lax.rem(y + 4 - ddy, 4) * 2 + other


def split(value):
    high = value.astype(jnp.bfloat16)
    return high, (value - high.astype(jnp.float32)).astype(jnp.bfloat16)


def one_hot(lanes, count):
    width = lanes.shape[1]
    rows = lax.broadcasted_iota(jnp.int32, (count, width), 0).astype(jnp.float32)
    return jnp.where(rows == lanes, 1.0, 0.0).astype(jnp.bfloat16)


def send(src, dst, send_sem, recv_sem, device):
    pltpu.make_async_remote_copy(
        src_ref=src, dst_ref=dst, send_sem=send_sem, recv_sem=recv_sem, device_id=device, device_id_type=MESH
    ).start()


def wait(ref, sem):
    pltpu.make_async_copy(ref, ref, sem).wait()


def kernel(
    blocks, ids, one_hbm, two_hbm, three_hbm, target_one, target_two, target_three, weights,
    graph, relative,
    fine, maps_out, maps_in, tags_out, tags_in, zags_out, zags_in, projected, coarse_one, out_two, in_two,
    size_two, sizein_two, spread, coarse_two, out_three, in_three, size_three, sizein_three, weighted,
    one, two, three, tables_sem, fine_send, fine_recv, maps_sem, tags_sem, zags_sem, two_sem, sizetwo_sem, three_sem, sizethree_sem,
):
    g, v = lax.axis_index("grp"), lax.axis_index("dev")
    barrier = pltpu.get_barrier_semaphore()
    for step in ORDER:
        pl.semaphore_signal(barrier, inc=1, device_id=(g, dest_of(v, *step)), device_id_type=MESH)
    for step in RING:
        pl.semaphore_signal(barrier, inc=1, device_id=(lax.rem(g + step, 8), v), device_id_type=MESH)
    tables = [
        pltpu.make_async_copy(source, table, tables_sem.at[place])
        for place, (source, table) in enumerate(((one_hbm, one), (two_hbm, two), (three_hbm, three)))
    ]
    for table in tables:
        table.start()
    mine = pltpu.make_async_copy(blocks.at[pl.ds(v * 4, 4)], fine.at[pl.ds(v * 4, 4)], fine_recv.at[v])
    mine.start()

    def send_fine(place):
        w = dest_of(v, *ORDER[place])
        send(
            blocks.at[pl.ds(w * 4, 4)], fine.at[pl.ds(v * 4, 4)], fine_send.at[place], fine_recv.at[v], (g, w)
        )

    pl.semaphore_wait(barrier, len(ORDER) + len(RING))
    for place in range(FIRST):
        send_fine(place)
    for table in tables:
        table.wait()

    def composed(numbers):
        first = jnp.concatenate([one[pl.ds(n, 1), :] for n in numbers], axis=0)
        second = jnp.concatenate([two[pl.ds(n // 2, 1), :] for n in numbers], axis=0)
        third = jnp.concatenate([three[pl.ds(n // 4, 1), :] for n in numbers], axis=0)
        second = jnp.take_along_axis(second, first, axis=1)
        return jnp.take_along_axis(third, second, axis=1).astype(jnp.float32)

    def make_maps(w, carry):
        numbers = [ids[a, w * 4 + j] for a in range(2) for j in range(4)]
        maps_out[w] = composed(numbers).astype(jnp.bfloat16)
        return carry

    lax.fori_loop(0, 32, make_maps, 0)
    maps_in[v] = maps_out[v]

    lane = lax.broadcasted_iota(jnp.int32, (32, BLOCK), 1)
    row = lax.broadcasted_iota(jnp.int32, (32, BLOCK), 0)
    local = weights[...]
    partial = jnp.sum(jnp.sum(local, axis=0, keepdims=True), axis=1, keepdims=True)

    def spread_tags(table, per, rows, lanes, place):
        table = jnp.concatenate([table] * (BLOCK // table.shape[1]), axis=1)
        table = jnp.broadcast_to(table, lanes.shape)
        picked = jnp.take_along_axis(table, rows * per + lax.rem(lanes, per), axis=1)
        return jnp.where(lanes // per == place, picked, 0).astype(jnp.float32)

    tags_one = spread_tags(target_one[...], 4, row, lane, v)
    tags_two = spread_tags(target_two[...], 2, row, lane, v)
    tags_two = tags_two + jnp.where(lane == v + 64, partial, 0.0)
    for w in range(32):
        tags_out[w, 0:1, :] = tags_one[w : w + 1]
        tags_out[w, 1:2, :] = tags_two[w : w + 1]
    tags_in[v] = tags_out[v]

    for step in ORDER:
        w = dest_of(v, *step)
        send(maps_out.at[w], maps_in.at[v], maps_sem.at[0], maps_sem.at[1], (g, w))
        send(tags_out.at[w], tags_in.at[v], tags_sem.at[0], tags_sem.at[1], (g, w))
    for place in range(FIRST, len(ORDER)):
        send_fine(place)

    base = (g * 32 + v) * 8
    own = composed([base + e for e in range(8)])
    part = lax.broadcasted_iota(jnp.int32, (8, BLOCK), 0)
    total_here = jnp.zeros((8, BLOCK), jnp.float32)
    up = lax.broadcasted_iota(jnp.int32, (BLOCK, BLOCK), 0).astype(jnp.float32)
    for e in range(8):
        hot = jnp.where(up == own[e : e + 1], 1.0, 0.0)
        total_here = total_here + lax.dot_general(
            jnp.where(part == e, local, 0.0), hot, (((1,), (1,)), ((), ())),
            precision=lax.Precision.HIGHEST, preferred_element_type=jnp.float32,
        )
    weighted[...] = jnp.sum(total_here, axis=0, keepdims=True)

    wait(maps_in.at[pl.ds(0, 31)], maps_sem.at[1])
    wait(tags_in.at[pl.ds(0, 31)], tags_sem.at[1])

    tags = jnp.sum(tags_in[...], axis=0)
    hot_one = one_hot(tags[0:1], 64)
    hot_one = jnp.concatenate([hot_one, hot_one], axis=1)
    hot_two = one_hot(tags[1:2], 32)[:, :64]
    hot_two = jnp.concatenate([hot_two, hot_two], axis=1)
    beyond = lax.broadcasted_iota(jnp.int32, (1, BLOCK), 1)
    group_total = jnp.sum(jnp.where(beyond >= 64, tags[1:2], 0.0), axis=1, keepdims=True)

    lane8 = lax.broadcasted_iota(jnp.int32, (8, BLOCK), 1)
    row8 = lax.broadcasted_iota(jnp.int32, (8, BLOCK), 0)
    tags_three = spread_tags(target_three[...], 4, row8, lane8, g)
    totals = jnp.where(beyond == g, group_total, 0.0)
    for h in range(8):
        zags_out[h, 0:1, :] = tags_three[h : h + 1]
        zags_out[h, 1:2, :] = totals
    zags_in[g] = zags_out[g]
    for step in RING:
        h = lax.rem(g + step, 8)
        send(zags_out.at[h], zags_in.at[g], zags_sem.at[0], zags_sem.at[1], (h, v))

    def project(turn, carry):
        s = source_of(v, turn)
        wait(fine.at[pl.ds(s * 4, 4)], fine_recv.at[s])
        maps = maps_in[s].astype(jnp.float32)
        for j in range(4):
            left = one_hot(maps[j : j + 1], BLOCK)
            right = one_hot(maps[4 + j : 5 + j], BLOCK)
            halfway = jnp.dot(left, fine[s * 4 + j], preferred_element_type=jnp.float32)
            both = jnp.concatenate(split(halfway), axis=0)
            full = lax.dot_general(
                both, right, (((1,), (1,)), ((), ())), preferred_element_type=jnp.float32
            )
            start = pl.multiple_of((s * 4 + j) * PITCH, 8)
            projected[pl.ds(start, BLOCK), :] = full[:BLOCK] + full[BLOCK:]
        return carry

    lax.fori_loop(0, 32, project, 0)

    def quantize(source, count, per, chunk, out, size):
        def one_group(w, carry):
            values = [
                source[pl.ds(pl.multiple_of((w * per + k) * PITCH + chunk * ROWS, 8), ROWS), :] for k in range(per)
            ]
            top = functools.reduce(jnp.maximum, [jnp.max(jnp.abs(a), axis=0, keepdims=True) for a in values])
            top = jnp.maximum(top, TINY)
            factor = TOP / top
            for k, a in enumerate(values):
                out[chunk, w * per + k] = jnp.round(a * factor).astype(jnp.int32).astype(jnp.int16)
            size[chunk, w] = top * (1.0 / TOP)
            return carry

        lax.fori_loop(0, count, one_group, 0, unroll=2)

    def restore(source, size, count, per, chunk):
        def one_group(w, carry):
            for k in range(per):
                s = w * per + k
                value = source[chunk, s].astype(jnp.int32).astype(jnp.float32)
                spread[pl.ds(pl.multiple_of(s * SPAN, 8), ROWS), :] = value * size[chunk, w]
            return carry

        lax.fori_loop(0, count, one_group, 0, unroll=2)

    def add_up(source, pitch, count, first, hot, store):
        def one_row(m, carry):
            value = source[pl.ds(first + m, count, stride=pitch), :]
            both = jnp.concatenate(split(value), axis=0)
            store(m, jnp.dot(hot, both, preferred_element_type=jnp.float32))
            return carry

        lax.fori_loop(0, ROWS, one_row, 0, unroll=8)

    def make_two(chunk):
        def keep(m, value):
            coarse_one[pl.ds(chunk * ROWS + m, 64, stride=PITCH), :] = value

        add_up(projected, PITCH, BLOCK, chunk * ROWS, hot_one, keep)
        quantize(coarse_one, 32, 2, chunk, out_two, size_two)
        here = pl.ds(v * 2, 2)
        in_two[chunk, here] = out_two[chunk, here]
        sizein_two[chunk, v] = size_two[chunk, v]

    def sends_two(chunk, step):
        w = dest_of(v, *step)
        send(
            size_two.at[chunk, w], sizein_two.at[chunk, v],
            sizetwo_sem.at[0, chunk], sizetwo_sem.at[1, chunk], (g, w),
        )
        send(
            out_two.at[chunk, pl.ds(w * 2, 2)], in_two.at[chunk, pl.ds(v * 2, 2)],
            two_sem.at[0, chunk], two_sem.at[1, chunk], (g, w),
        )

    def make_three(chunk):
        def keep(m, value):
            coarse_two[pl.ds(chunk * ROWS + m, 32, stride=PITCH), :] = value

        wait(sizein_two.at[chunk, pl.ds(0, 31)], sizetwo_sem.at[1, chunk])
        wait(in_two.at[chunk, pl.ds(0, 62)], two_sem.at[1, chunk])
        restore(in_two, sizein_two, 32, 2, chunk)
        add_up(spread, SPAN, 64, 0, hot_two, keep)
        quantize(coarse_two, 8, 4, chunk, out_three, size_three)
        here = pl.ds(g * 4, 4)
        in_three[chunk, here] = out_three[chunk, here]
        sizein_three[chunk, g] = size_three[chunk, g]

    def sends_three(chunk, step):
        h = lax.rem(g + step, 8)
        send(
            size_three.at[chunk, h], sizein_three.at[chunk, g],
            sizethree_sem.at[0, chunk], sizethree_sem.at[1, chunk], (h, v),
        )
        send(
            out_three.at[chunk, pl.ds(h * 4, 4)], in_three.at[chunk, pl.ds(g * 4, 4)],
            three_sem.at[0, chunk], three_sem.at[1, chunk], (h, v),
        )

    for chunk in range(AHEAD):
        make_two(chunk)
        for step in ORDER:
            sends_two(chunk, step)
    wait(zags_in.at[pl.ds(0, 7)], zags_sem.at[1])
    zags = jnp.sum(zags_in[...], axis=0)
    hot_three = one_hot(zags[0:1], 16)[:, :32]
    hot_three = jnp.concatenate([hot_three, hot_three], axis=1)
    relative[...] = weighted[...] * 32768.0 / jnp.sum(zags[1:2], axis=1, keepdims=True)
    for chunk in range(CHUNKS):
        ahead = chunk + AHEAD
        if ahead < CHUNKS:
            make_two(ahead)
        make_three(chunk)
        for place, step in enumerate(ORDER if ahead < CHUNKS else RING * 4):
            if place % 4 == 0 and place // 4 < len(RING):
                sends_three(chunk, RING[place // 4])
            if ahead < CHUNKS:
                sends_two(ahead, step)

    for chunk in range(CHUNKS):
        wait(sizein_three.at[chunk, pl.ds(0, 7)], sizethree_sem.at[1, chunk])
        wait(in_three.at[chunk, pl.ds(0, 28)], three_sem.at[1, chunk])
        restore(in_three, sizein_three, 8, 4, chunk)

        def keep_three(m, value, chunk=chunk):
            graph[pl.ds(chunk * ROWS + m, 16, stride=BLOCK), :] = value

        add_up(spread, SPAN, 32, 0, hot_three, keep_three)

    for place, step in enumerate(ORDER):
        w = dest_of(v, *step)
        wait(blocks.at[pl.ds(w * 4, 4)], fine_send.at[place])
    wait(maps_in.at[pl.ds(0, 31)], maps_sem.at[0])
    wait(tags_in.at[pl.ds(0, 31)], tags_sem.at[0])
    wait(zags_in.at[pl.ds(0, 7)], zags_sem.at[0])
    for chunk in range(CHUNKS):
        wait(size_two.at[chunk, pl.ds(0, 31)], sizetwo_sem.at[0, chunk])
        wait(out_two.at[chunk, pl.ds(0, 62)], two_sem.at[0, chunk])
        wait(size_three.at[chunk, pl.ds(0, 7)], sizethree_sem.at[0, chunk])
        wait(out_three.at[chunk, pl.ds(0, 28)], three_sem.at[0, chunk])


def per_device(
    blocks, ids_one, ids_two, ids_three, match_one, match_two, match_three,
    target_one, target_two, target_three, vertex_weights,
):
    del ids_two, ids_three
    vmem = pl.BlockSpec(memory_space=pltpu.VMEM)
    hbm = pl.BlockSpec(memory_space=pl.ANY)
    f32, i16, bf16 = jnp.float32, jnp.int16, jnp.bfloat16
    graph, relative = pl.pallas_call(
        kernel,
        out_shape=(
            jax.ShapeDtypeStruct((16 * BLOCK, BLOCK), f32),
            jax.ShapeDtypeStruct((1, BLOCK), f32),
        ),
        in_specs=[hbm, pl.BlockSpec(memory_space=pltpu.SMEM), hbm, hbm, hbm] + [vmem] * 4,
        out_specs=(vmem, vmem),
        scratch_shapes=[
            pltpu.VMEM((128, BLOCK, BLOCK), bf16),
            pltpu.VMEM((32, 8, BLOCK), bf16),
            pltpu.VMEM((32, 8, BLOCK), bf16),
            pltpu.VMEM((32, 2, BLOCK), f32),
            pltpu.VMEM((32, 2, BLOCK), f32),
            pltpu.VMEM((8, 2, BLOCK), f32),
            pltpu.VMEM((8, 2, BLOCK), f32),
            pltpu.VMEM((128 * PITCH, BLOCK), f32),
            pltpu.VMEM((64 * PITCH, BLOCK), f32),
            pltpu.VMEM((CHUNKS, 64, ROWS, BLOCK), i16),
            pltpu.VMEM((CHUNKS, 64, ROWS, BLOCK), i16),
            pltpu.VMEM((CHUNKS, 32, 1, BLOCK), f32),
            pltpu.VMEM((CHUNKS, 32, 1, BLOCK), f32),
            pltpu.VMEM((64 * SPAN, BLOCK), f32),
            pltpu.VMEM((32 * PITCH, BLOCK), f32),
            pltpu.VMEM((CHUNKS, 32, ROWS, BLOCK), i16),
            pltpu.VMEM((CHUNKS, 32, ROWS, BLOCK), i16),
            pltpu.VMEM((CHUNKS, 8, 1, BLOCK), f32),
            pltpu.VMEM((CHUNKS, 8, 1, BLOCK), f32),
            pltpu.VMEM((1, BLOCK), f32),
            pltpu.VMEM(match_one.shape, jnp.int32),
            pltpu.VMEM(match_two.shape, jnp.int32),
            pltpu.VMEM(match_three.shape, jnp.int32),
            pltpu.SemaphoreType.DMA((3,)),
            pltpu.SemaphoreType.DMA((31,)),
            pltpu.SemaphoreType.DMA((32,)),
            pltpu.SemaphoreType.DMA((2,)),
            pltpu.SemaphoreType.DMA((2,)),
            pltpu.SemaphoreType.DMA((2,)),
            pltpu.SemaphoreType.DMA((2, CHUNKS)),
            pltpu.SemaphoreType.DMA((2, CHUNKS)),
            pltpu.SemaphoreType.DMA((2, CHUNKS)),
            pltpu.SemaphoreType.DMA((2, CHUNKS)),
        ],
        compiler_params=pltpu.CompilerParams(
            collective_id=0, has_side_effects=True, vmem_limit_bytes=56 * 2**20
        ),
        name="coarsen",
    )(
        blocks, ids_one, match_one, match_two, match_three,
        target_one.reshape(1, -1), target_two.reshape(1, -1), target_three.reshape(1, -1), vertex_weights,
    )
    return graph.reshape(16, BLOCK, BLOCK), relative


def solution(mesh):
    both = ("grp", "dev")
    in_specs = (
        P(both, None, None), P(None, both), P(None, both), P(None, both), P(), P(), P(),
        P(both), P(both), P(both), P(both, None),
    )
    return jax.shard_map(
        per_device, mesh=mesh, in_specs=in_specs, out_specs=(P(both, None, None), P(both, None)), check_vma=False
    )
```

time: 123 us -> 107 us (0.87)
  the two profiles are of different devices: /device:TPU:2 before, /device:TPU:1 now
where the time goes in v2:
time: 107 us; the launch traced here: 106 us
  Pallas kernels  102 us (95%)
  local copies, waits for them, and re-layouts  3.41 us (3%)
    pallas_call x1, Pallas kernels, per_device(): pl.pallas_call(kernel, out_shape=(jax.ShapeDtypeStruct((16 * BLOCK, BLOCK...  102 us
    unnamed x2, local copies, waits for them, and re-layouts  3.41 us

profile of v2, /device:TPU:1, one launch (start us, length us, event | category | flops | bytes accessed | tf_op | source)
XLA Modules:
  0.0 106.1 jit_solution(12138588402403292949)
XLA Ops:
  0.6 102.0 %coarsen.1 = (f32[2048,128]{1,0:T(8,128)}, f32[1,128]{1,0:T(1,128)}) custom-call(bf16[128,128,128]{2,1,0:T(8,128)(2,1)} %blocks.1, s32[2,128]{1,0:T(2,128)} %ids.1, s32[2048,128]{1,0:T(8,128)} %one_hbm.1, s32[1024,128]{1,0:T(8,128)} %two_hbm.1, s32[512,128]{1,0:T(8,128)} %three_hbm.1, s32[1,128]{1,0:T(1,128)} %bitcast.5, s32[1,64]{1,0:T(1,128)} %bitcast.6, ...), custom_call_target="tpu_custom_call" | custom-call | tf_op jit(solution)/shard_map/coarsen/pallas_call | solution.py:333
  102.7 2.3 %copy.13 = f32[16,128,128]{2,1,0:T(8,128)} copy(f32[16,128,128]{2,1,0:T(8,128)} %bitcast.4) | data formatting | bytes 2097152
  105.0 1.1 %copy.14 = f32[1,128]{1,0:T(1,128)} copy(f32[1,128]{1,0:T(1,128)} %get-tuple-element.9) | data formatting | bytes 1024

commit v3 on v2

--- a/solution.py
+++ b/solution.py
@@ -9,10 +9,10 @@
 
 MESH = pl.DeviceIdType.MESH
 BLOCK = 128
-PITCH = 136
 CHUNKS = 8
+EARLY = 4
 AHEAD = 3
-FIRST = 5
+HALF = BLOCK // 2
 ROWS = BLOCK // CHUNKS
 SPAN = ROWS + 8
 TOP = 32767.0
@@ -38,16 +38,11 @@
     return lax.rem(x + ddx, 4) * 8 + lax.rem(y + ddy, 4) * 2 + lax.rem(c + dc, 2)
 
 
-def source_of(v, turn):
+def dest_at(v, turn):
     code = jnp.int32(0)
     for place, (dx, dy, dc) in enumerate(ORDER):
         code = jnp.where(turn == place + 1, dx * 8 + dy * 2 + dc, code)
-    dx, dy, dc = code // 8, lax.rem(code // 2, 4), lax.rem(code, 2)
-    x, y, c = v // 8, lax.rem(v // 2, 4), lax.rem(v, 2)
-    other = lax.rem(c + dc, 2)
-    ddx = jnp.where(other == 1, dy, dx)
-    ddy = jnp.where(other == 1, dx, dy)
-    return lax.rem(x + 4 - ddx, 4) * 8 + lax.rem(y + 4 - ddy, 4) * 2 + other
+    return dest_of(v, code // 8, lax.rem(code // 2, 4), lax.rem(code, 2))
 
 
 def split(value):
@@ -74,9 +69,10 @@
 def kernel(
     blocks, ids, one_hbm, two_hbm, three_hbm, target_one, target_two, target_three, weights,
     graph, relative,
-    fine, maps_out, maps_in, tags_out, tags_in, zags_out, zags_in, projected, coarse_one, out_two, in_two,
+    fine, out_one, in_one, size_one, sizein_one, tags_out, tags_in, zags_out, zags_in, coarse_one, out_two, in_two,
     size_two, sizein_two, spread, coarse_two, out_three, in_three, size_three, sizein_three, weighted,
-    one, two, three, tables_sem, fine_send, fine_recv, maps_sem, tags_sem, zags_sem, two_sem, sizetwo_sem, three_sem, sizethree_sem,
+    one, two, three, maps, projected, tables_sem, fine_sem, one_sem, sizeone_sem, tags_sem, zags_sem,
+    two_sem, sizetwo_sem, three_sem, sizethree_sem,
 ):
     g, v = lax.axis_index("grp"), lax.axis_index("dev")
     barrier = pltpu.get_barrier_semaphore()
@@ -90,20 +86,9 @@
     ]
     for table in tables:
         table.start()
-    mine = pltpu.make_async_copy(blocks.at[pl.ds(v * 4, 4)], fine.at[pl.ds(v * 4, 4)], fine_recv.at[v])
-    mine.start()
-
-    def send_fine(place):
-        w = dest_of(v, *ORDER[place])
-        send(
-            blocks.at[pl.ds(w * 4, 4)], fine.at[pl.ds(v * 4, 4)], fine_send.at[place], fine_recv.at[v], (g, w)
-        )
-
-    pl.semaphore_wait(barrier, len(ORDER) + len(RING))
-    for place in range(FIRST):
-        send_fine(place)
-    for table in tables:
-        table.wait()
+    for place, step in enumerate(((0, 0, 0),) + ORDER):
+        some = pl.ds(dest_of(v, *step) * 4, 4)
+        pltpu.make_async_copy(blocks.at[some], fine.at[some], fine_sem.at[place]).start()
 
     def composed(numbers):
         first = jnp.concatenate([one[pl.ds(n, 1), :] for n in numbers], axis=0)
@@ -111,14 +96,6 @@
         third = jnp.concatenate([three[pl.ds(n // 4, 1), :] for n in numbers], axis=0)
         second = jnp.take_along_axis(second, first, axis=1)
         return jnp.take_along_axis(third, second, axis=1).astype(jnp.float32)
-
-    def make_maps(w, carry):
-        numbers = [ids[a, w * 4 + j] for a in range(2) for j in range(4)]
-        maps_out[w] = composed(numbers).astype(jnp.bfloat16)
-        return carry
-
-    lax.fori_loop(0, 32, make_maps, 0)
-    maps_in[v] = maps_out[v]
 
     lane = lax.broadcasted_iota(jnp.int32, (32, BLOCK), 1)
     row = lax.broadcasted_iota(jnp.int32, (32, BLOCK), 0)
@@ -139,12 +116,75 @@
         tags_out[w, 1:2, :] = tags_two[w : w + 1]
     tags_in[v] = tags_out[v]
 
+    for table in tables:
+        table.wait()
+
+    def find_maps(turn):
+        w = dest_at(v, turn)
+        maps[...] = composed([ids[a, w * 4 + j] for a in range(2) for j in range(4)])
+
+    def project(turn):
+        w = dest_at(v, turn)
+        wait(fine.at[pl.ds(w * 4, 4)], fine_sem.at[turn])
+        here = maps[...]
+        for j in range(4):
+            left = one_hot(here[j : j + 1], BLOCK)
+            right = one_hot(here[4 + j : 5 + j], BLOCK)
+            halfway = jnp.dot(left, fine[w * 4 + j], preferred_element_type=jnp.float32)
+            both = jnp.concatenate(split(halfway), axis=0)
+            full = lax.dot_general(both, right, (((1,), (1,)), ((), ())), preferred_element_type=jnp.float32)
+            projected[j * BLOCK : (j + 1) * BLOCK, :] = full[:BLOCK] + full[BLOCK:]
+
+    def round_one(turn):
+        w = dest_at(v, turn)
+        for pair in range(2):
+            for half in range(2):
+                starts = [(pair * 2 + k) * BLOCK + half * HALF for k in range(2)]
+                values = [projected[start : start + HALF, :] for start in starts]
+                top = jnp.maximum(*[jnp.max(jnp.abs(a), axis=0, keepdims=True) for a in values])
+                top = jnp.maximum(top, TINY)
+                factor = TOP / top
+                for k, a in enumerate(values):
+                    out_one[half, w * 4 + pair * 2 + k] = jnp.round(a * factor).astype(jnp.int32).astype(jnp.int16)
+                size_one[half, w, pair : pair + 1, :] = top * (1.0 / TOP)
+
+    def send_one(half, turn):
+        w = dest_at(v, turn)
+        send(
+            size_one.at[half, w], sizein_one.at[half, v], sizeone_sem.at[0, half], sizeone_sem.at[1, half], (g, w)
+        )
+        send(
+            out_one.at[half, pl.ds(w * 4, 4)], in_one.at[half, pl.ds(v * 4, 4)],
+            one_sem.at[0, half], one_sem.at[1, half], (g, w),
+        )
+
+    find_maps(0)
+    project(0)
+    find_maps(1)
+    pl.semaphore_wait(barrier, len(ORDER) + len(RING))
     for step in ORDER:
         w = dest_of(v, *step)
-        send(maps_out.at[w], maps_in.at[v], maps_sem.at[0], maps_sem.at[1], (g, w))
         send(tags_out.at[w], tags_in.at[v], tags_sem.at[0], tags_sem.at[1], (g, w))
-    for place in range(FIRST, len(ORDER)):
-        send_fine(place)
+
+    def step_on(turn, carry):
+        round_one(turn - 1)
+        project(turn)
+        find_maps(jnp.minimum(turn + 1, 31))
+
+        @pl.when(turn >= 3)
+        def _():
+            send_one(0, turn - 2)
+
+        return carry
+
+    lax.fori_loop(1, 32, step_on, 0)
+    send_one(0, 30)
+    round_one(31)
+    send_one(0, 31)
+    lax.fori_loop(1, 32, lambda turn, carry: (send_one(1, turn), carry)[1], 0)
+    for half in range(2):
+        in_one[half, pl.ds(v * 4, 4)] = out_one[half, pl.ds(v * 4, 4)]
+        sizein_one[half, v] = size_one[half, v]
 
     base = (g * 32 + v) * 8
     own = composed([base + e for e in range(8)])
@@ -159,9 +199,7 @@
         )
     weighted[...] = jnp.sum(total_here, axis=0, keepdims=True)
 
-    wait(maps_in.at[pl.ds(0, 31)], maps_sem.at[1])
     wait(tags_in.at[pl.ds(0, 31)], tags_sem.at[1])
-
     tags = jnp.sum(tags_in[...], axis=0)
     hot_one = one_hot(tags[0:1], 64)
     hot_one = jnp.concatenate([hot_one, hot_one], axis=1)
@@ -182,28 +220,10 @@
         h = lax.rem(g + step, 8)
         send(zags_out.at[h], zags_in.at[g], zags_sem.at[0], zags_sem.at[1], (h, v))
 
-    def project(turn, carry):
-        s = source_of(v, turn)
-        wait(fine.at[pl.ds(s * 4, 4)], fine_recv.at[s])
-        maps = maps_in[s].astype(jnp.float32)
-        for j in range(4):
-            left = one_hot(maps[j : j + 1], BLOCK)
-            right = one_hot(maps[4 + j : 5 + j], BLOCK)
-            halfway = jnp.dot(left, fine[s * 4 + j], preferred_element_type=jnp.float32)
-            both = jnp.concatenate(split(halfway), axis=0)
-            full = lax.dot_general(
-                both, right, (((1,), (1,)), ((), ())), preferred_element_type=jnp.float32
-            )
-            start = pl.multiple_of((s * 4 + j) * PITCH, 8)
-            projected[pl.ds(start, BLOCK), :] = full[:BLOCK] + full[BLOCK:]
-        return carry
-
-    lax.fori_loop(0, 32, project, 0)
-
     def quantize(source, count, per, chunk, out, size):
         def one_group(w, carry):
             values = [
-                source[pl.ds(pl.multiple_of((w * per + k) * PITCH + chunk * ROWS, 8), ROWS), :] for k in range(per)
+                source[pl.ds(pl.multiple_of((w * per + k) * SPAN, 8), ROWS), :] for k in range(per)
             ]
             top = functools.reduce(jnp.maximum, [jnp.max(jnp.abs(a), axis=0, keepdims=True) for a in values])
             top = jnp.maximum(top, TINY)
@@ -225,20 +245,38 @@
 
         lax.fori_loop(0, count, one_group, 0, unroll=2)
 
-    def add_up(source, pitch, count, first, hot, store):
+    def add_up(source, pitch, count, hot, store):
         def one_row(m, carry):
-            value = source[pl.ds(first + m, count, stride=pitch), :]
+            value = source[pl.ds(m, count, stride=pitch), :]
             both = jnp.concatenate(split(value), axis=0)
             store(m, jnp.dot(hot, both, preferred_element_type=jnp.float32))
             return carry
 
         lax.fori_loop(0, ROWS, one_row, 0, unroll=8)
 
+    def restore_one(chunk):
+        half, first = chunk * ROWS // HALF, chunk * ROWS % HALF
+
+        def one_source(w, carry):
+            for pair in range(2):
+                size = sizein_one[half, w, pair : pair + 1, :]
+                for s in (w * 4 + pair * 2, w * 4 + pair * 2 + 1):
+                    value = in_one[half, s, first : first + ROWS, :].astype(jnp.int32).astype(jnp.float32)
+                    spread[pl.ds(pl.multiple_of(s * SPAN, 8), ROWS), :] = value * size
+            return carry
+
+        lax.fori_loop(0, 32, one_source, 0, unroll=2)
+
     def make_two(chunk):
         def keep(m, value):
-            coarse_one[pl.ds(chunk * ROWS + m, 64, stride=PITCH), :] = value
-
-        add_up(projected, PITCH, BLOCK, chunk * ROWS, hot_one, keep)
+            coarse_one[pl.ds(m, 64, stride=SPAN), :] = value
+
+        if chunk * ROWS % HALF == 0:
+            half = chunk * ROWS // HALF
+            wait(sizein_one.at[half, pl.ds(0, 31)], sizeone_sem.at[1, half])
+            wait(in_one.at[half, pl.ds(0, 124)], one_sem.at[1, half])
+        restore_one(chunk)
+        add_up(spread, SPAN, 128, hot_one, keep)
         quantize(coarse_one, 32, 2, chunk, out_two, size_two)
         here = pl.ds(v * 2, 2)
         in_two[chunk, here] = out_two[chunk, here]
@@ -257,12 +295,12 @@
 
     def make_three(chunk):
         def keep(m, value):
-            coarse_two[pl.ds(chunk * ROWS + m, 32, stride=PITCH), :] = value
+            coarse_two[pl.ds(m, 32, stride=SPAN), :] = value
 
         wait(sizein_two.at[chunk, pl.ds(0, 31)], sizetwo_sem.at[1, chunk])
         wait(in_two.at[chunk, pl.ds(0, 62)], two_sem.at[1, chunk])
         restore(in_two, sizein_two, 32, 2, chunk)
-        add_up(spread, SPAN, 64, 0, hot_two, keep)
+        add_up(spread, SPAN, 64, hot_two, keep)
         quantize(coarse_two, 8, 4, chunk, out_three, size_three)
         here = pl.ds(g * 4, 4)
         in_three[chunk, here] = out_three[chunk, here]
@@ -279,10 +317,11 @@
             three_sem.at[0, chunk], three_sem.at[1, chunk], (h, v),
         )
 
-    for chunk in range(AHEAD):
+    for chunk in range(EARLY):
         make_two(chunk)
-        for step in ORDER:
-            sends_two(chunk, step)
+        if chunk < AHEAD:
+            for step in ORDER:
+                sends_two(chunk, step)
     wait(zags_in.at[pl.ds(0, 7)], zags_sem.at[1])
     zags = jnp.sum(zags_in[...], axis=0)
     hot_three = one_hot(zags[0:1], 16)[:, :32]
@@ -290,12 +329,12 @@
     relative[...] = weighted[...] * 32768.0 / jnp.sum(zags[1:2], axis=1, keepdims=True)
     for chunk in range(CHUNKS):
         ahead = chunk + AHEAD
-        if ahead < CHUNKS:
-            make_two(ahead)
+        if chunk + EARLY < CHUNKS:
+            make_two(chunk + EARLY)
         make_three(chunk)
         for place, step in enumerate(ORDER if ahead < CHUNKS else RING * 4):
-            if place % 4 == 0 and place // 4 < len(RING):
-                sends_three(chunk, RING[place // 4])
+            if place < len(RING):
+                sends_three(chunk, RING[place])
             if ahead < CHUNKS:
                 sends_two(ahead, step)
 
@@ -307,12 +346,11 @@
         def keep_three(m, value, chunk=chunk):
             graph[pl.ds(chunk * ROWS + m, 16, stride=BLOCK), :] = value
 
-        add_up(spread, SPAN, 32, 0, hot_three, keep_three)
-
-    for place, step in enumerate(ORDER):
-        w = dest_of(v, *step)
-        wait(blocks.at[pl.ds(w * 4, 4)], fine_send.at[place])
-    wait(maps_in.at[pl.ds(0, 31)], maps_sem.at[0])
+        add_up(spread, SPAN, 32, hot_three, keep_three)
+
+    for half in range(2):
+        wait(size_one.at[half, pl.ds(0, 31)], sizeone_sem.at[0, half])
+        wait(out_one.at[half, pl.ds(0, 124)], one_sem.at[0, half])
     wait(tags_in.at[pl.ds(0, 31)], tags_sem.at[0])
     wait(zags_in.at[pl.ds(0, 7)], zags_sem.at[0])
     for chunk in range(CHUNKS):
@@ -340,20 +378,21 @@
         out_specs=(vmem, vmem),
         scratch_shapes=[
             pltpu.VMEM((128, BLOCK, BLOCK), bf16),
-            pltpu.VMEM((32, 8, BLOCK), bf16),
-            pltpu.VMEM((32, 8, BLOCK), bf16),
+            pltpu.VMEM((2, 128, HALF, BLOCK), i16),
+            pltpu.VMEM((2, 128, HALF, BLOCK), i16),
+            pltpu.VMEM((2, 32, 2, BLOCK), f32),
+            pltpu.VMEM((2, 32, 2, BLOCK), f32),
             pltpu.VMEM((32, 2, BLOCK), f32),
             pltpu.VMEM((32, 2, BLOCK), f32),
             pltpu.VMEM((8, 2, BLOCK), f32),
             pltpu.VMEM((8, 2, BLOCK), f32),
-            pltpu.VMEM((128 * PITCH, BLOCK), f32),
-            pltpu.VMEM((64 * PITCH, BLOCK), f32),
+            pltpu.VMEM((64 * SPAN, BLOCK), f32),
             pltpu.VMEM((CHUNKS, 64, ROWS, BLOCK), i16),
             pltpu.VMEM((CHUNKS, 64, ROWS, BLOCK), i16),
             pltpu.VMEM((CHUNKS, 32, 1, BLOCK), f32),
             pltpu.VMEM((CHUNKS, 32, 1, BLOCK), f32),
-            pltpu.VMEM((64 * SPAN, BLOCK), f32),
-            pltpu.VMEM((32 * PITCH, BLOCK), f32),
+            pltpu.VMEM((128 * SPAN, BLOCK), f32),
+            pltpu.VMEM((32 * SPAN, BLOCK), f32),
             pltpu.VMEM((CHUNKS, 32, ROWS, BLOCK), i16),
             pltpu.VMEM((CHUNKS, 32, ROWS, BLOCK), i16),
             pltpu.VMEM((CHUNKS, 8, 1, BLOCK), f32),
@@ -362,10 +401,12 @@
             pltpu.VMEM(match_one.shape, jnp.int32),
             pltpu.VMEM(match_two.shape, jnp.int32),
             pltpu.VMEM(match_three.shape, jnp.int32),
+            pltpu.VMEM((8, BLOCK), f32),
+            pltpu.VMEM((4 * BLOCK, BLOCK), f32),
             pltpu.SemaphoreType.DMA((3,)),
-            pltpu.SemaphoreType.DMA((31,)),
             pltpu.SemaphoreType.DMA((32,)),
-            pltpu.SemaphoreType.DMA((2,)),
+            pltpu.SemaphoreType.DMA((2, 2)),
+            pltpu.SemaphoreType.DMA((2, 2)),
             pltpu.SemaphoreType.DMA((2,)),
             pltpu.SemaphoreType.DMA((2,)),
             pltpu.SemaphoreType.DMA((2, CHUNKS)),

time: 107 us -> 104 us (0.972)
  Pallas kernels: 102 us -> 99.7 us
    pallas_call x1, Pallas kernels: 102 us -> 99.7 us  [per_device(): pl.pallas_call(kernel, out_shape=(jax.ShapeDtypeStruct((16 * BLOCK, BLOCK...]
where the time goes in v3:
time: 104 us
  Pallas kernels  99.7 us (96%)
  local copies, waits for them, and re-layouts  3.41 us (3%)
    pallas_call x1, Pallas kernels, per_device(): pl.pallas_call(kernel, out_shape=(jax.ShapeDtypeStruct((16 * BLOCK, BLOCK...  99.7 us
    unnamed x2, local copies, waits for them, and re-layouts  3.41 us

profile of v3, /device:TPU:1, one launch (start us, length us, event | category | flops | bytes accessed | tf_op | source)
XLA Modules:
  0.0 103.8 jit_solution(16676114802213246045)
XLA Ops:
  0.6 99.7 %coarsen.1 = (f32[2048,128]{1,0:T(8,128)}, f32[1,128]{1,0:T(1,128)}) custom-call(bf16[128,128,128]{2,1,0:T(8,128)(2,1)} %blocks.1, s32[2,128]{1,0:T(2,128)} %ids.1, s32[2048,128]{1,0:T(8,128)} %one_hbm.1, s32[1024,128]{1,0:T(8,128)} %two_hbm.1, s32[512,128]{1,0:T(8,128)} %three_hbm.1, s32[1,128]{1,0:T(1,128)} %bitcast.5, s32[1,64]{1,0:T(1,128)} %bitcast.6, ...), custom_call_target="tpu_custom_call" | custom-call | tf_op jit(solution)/shard_map/coarsen/pallas_call | solution.py:371
  100.4 2.3 %copy.13 = f32[16,128,128]{2,1,0:T(8,128)} copy(f32[16,128,128]{2,1,0:T(8,128)} %bitcast.4) | data formatting | bytes 2097152
  102.6 1.1 %copy.14 = f32[1,128]{1,0:T(1,128)} copy(f32[1,128]{1,0:T(1,128)} %get-tuple-element.9) | data formatting | bytes 1024

commit v4 on v3

--- a/solution.py
+++ b/solution.py
@@ -17,13 +17,14 @@
 SPAN = ROWS + 8
 TOP = 32767.0
 TINY = 1e-30
+PARTS = 4
 ROUNDS = (
-    ((0, 0),),
+    ((2, 2),),
     ((0, 1), (1, 1), (0, 3), (3, 3)),
     ((1, 0), (1, 3), (3, 0), (3, 1)),
     ((0, 2), (2, 1), (2, 3)),
     ((2, 0), (1, 2), (3, 2)),
-    ((2, 2),),
+    ((0, 0),),
 )
 ORDER = tuple(
     (dx, dy, dc) for turn in ROUNDS for dc in (0, 1) for dx, dy in turn if (dx, dy, dc) != (0, 0, 0)
@@ -41,7 +42,7 @@
 def dest_at(v, turn):
     code = jnp.int32(0)
     for place, (dx, dy, dc) in enumerate(ORDER):
-        code = jnp.where(turn == place + 1, dx * 8 + dy * 2 + dc, code)
+        code = jnp.where(turn == place, dx * 8 + dy * 2 + dc, code)
     return dest_of(v, code // 8, lax.rem(code // 2, 4), lax.rem(code, 2))
 
 
@@ -86,7 +87,7 @@
     ]
     for table in tables:
         table.start()
-    for place, step in enumerate(((0, 0, 0),) + ORDER):
+    for place, step in enumerate(ORDER + ((0, 0, 0),)):
         some = pl.ds(dest_of(v, *step) * 4, 4)
         pltpu.make_async_copy(blocks.at[some], fine.at[some], fine_sem.at[place]).start()
 
@@ -96,25 +97,6 @@
         third = jnp.concatenate([three[pl.ds(n // 4, 1), :] for n in numbers], axis=0)
         second = jnp.take_along_axis(second, first, axis=1)
         return jnp.take_along_axis(third, second, axis=1).astype(jnp.float32)
-
-    lane = lax.broadcasted_iota(jnp.int32, (32, BLOCK), 1)
-    row = lax.broadcasted_iota(jnp.int32, (32, BLOCK), 0)
-    local = weights[...]
-    partial = jnp.sum(jnp.sum(local, axis=0, keepdims=True), axis=1, keepdims=True)
-
-    def spread_tags(table, per, rows, lanes, place):
-        table = jnp.concatenate([table] * (BLOCK // table.shape[1]), axis=1)
-        table = jnp.broadcast_to(table, lanes.shape)
-        picked = jnp.take_along_axis(table, rows * per + lax.rem(lanes, per), axis=1)
-        return jnp.where(lanes // per == place, picked, 0).astype(jnp.float32)
-
-    tags_one = spread_tags(target_one[...], 4, row, lane, v)
-    tags_two = spread_tags(target_two[...], 2, row, lane, v)
-    tags_two = tags_two + jnp.where(lane == v + 64, partial, 0.0)
-    for w in range(32):
-        tags_out[w, 0:1, :] = tags_one[w : w + 1]
-        tags_out[w, 1:2, :] = tags_two[w : w + 1]
-    tags_in[v] = tags_out[v]
 
     for table in tables:
         table.wait()
@@ -162,26 +144,39 @@
     project(0)
     find_maps(1)
     pl.semaphore_wait(barrier, len(ORDER) + len(RING))
-    for step in ORDER:
-        w = dest_of(v, *step)
-        send(tags_out.at[w], tags_in.at[v], tags_sem.at[0], tags_sem.at[1], (g, w))
-
     def step_on(turn, carry):
         round_one(turn - 1)
         project(turn)
         find_maps(jnp.minimum(turn + 1, 31))
-
-        @pl.when(turn >= 3)
-        def _():
-            send_one(0, turn - 2)
-
+        send_one(0, turn - 1)
         return carry
 
     lax.fori_loop(1, 32, step_on, 0)
-    send_one(0, 30)
     round_one(31)
-    send_one(0, 31)
-    lax.fori_loop(1, 32, lambda turn, carry: (send_one(1, turn), carry)[1], 0)
+
+    lane = lax.broadcasted_iota(jnp.int32, (32, BLOCK), 1)
+    row = lax.broadcasted_iota(jnp.int32, (32, BLOCK), 0)
+    local = weights[...]
+    partial = jnp.sum(jnp.sum(local, axis=0, keepdims=True), axis=1, keepdims=True)
+
+    def spread_tags(table, per, rows, lanes, place):
+        table = jnp.concatenate([table] * (BLOCK // table.shape[1]), axis=1)
+        table = jnp.broadcast_to(table, lanes.shape)
+        picked = jnp.take_along_axis(table, rows * per + lax.rem(lanes, per), axis=1)
+        return jnp.where(lanes // per == place, picked, 0).astype(jnp.float32)
+
+    tags_one = spread_tags(target_one[...], 4, row, lane, v)
+    tags_two = spread_tags(target_two[...], 2, row, lane, v)
+    tags_two = tags_two + jnp.where(lane == v + 64, partial, 0.0)
+    for w in range(32):
+        tags_out[w, 0:1, :] = tags_one[w : w + 1]
+        tags_out[w, 1:2, :] = tags_two[w : w + 1]
+    tags_in[v] = tags_out[v]
+
+    for step in ORDER:
+        w = dest_of(v, *step)
+        send(tags_out.at[w], tags_in.at[v], tags_sem.at[0], tags_sem.at[1], (g, w))
+    lax.fori_loop(0, 31, lambda turn, carry: (send_one(1, turn), carry)[1], 0)
     for half in range(2):
         in_one[half, pl.ds(v * 4, 4)] = out_one[half, pl.ds(v * 4, 4)]
         sizein_one[half, v] = size_one[half, v]
@@ -358,6 +353,23 @@
         wait(out_two.at[chunk, pl.ds(0, 62)], two_sem.at[0, chunk])
         wait(size_three.at[chunk, pl.ds(0, 7)], sizethree_sem.at[0, chunk])
         wait(out_three.at[chunk, pl.ds(0, 28)], three_sem.at[0, chunk])
+
+
+def copy_kernel(graph, relative, graph_out, relative_out, held, in_sem, out_sem):
+    part = graph.shape[0] // PARTS
+    ins, outs = [], []
+    for place in range(PARTS):
+        here = pl.ds(place * part, part)
+        ins.append(pltpu.make_async_copy(graph.at[here], held.at[here], in_sem.at[place]))
+        outs.append(pltpu.make_async_copy(held.at[here], graph_out.at[here], out_sem.at[place]))
+    for copy in ins:
+        copy.start()
+    relative_out[...] = relative[...]
+    for before, after in zip(ins, outs):
+        before.wait()
+        after.start()
+    for copy in outs:
+        copy.wait()
 
 
 def per_device(
@@ -422,6 +434,18 @@
         blocks, ids_one, match_one, match_two, match_three,
         target_one.reshape(1, -1), target_two.reshape(1, -1), target_three.reshape(1, -1), vertex_weights,
     )
+    graph, relative = pl.pallas_call(
+        copy_kernel,
+        out_shape=(jax.ShapeDtypeStruct(graph.shape, f32), jax.ShapeDtypeStruct(relative.shape, f32)),
+        in_specs=[hbm, vmem],
+        out_specs=(hbm, vmem),
+        scratch_shapes=[
+            pltpu.VMEM(graph.shape, f32),
+            pltpu.SemaphoreType.DMA((PARTS,)),
+            pltpu.SemaphoreType.DMA((PARTS,)),
+        ],
+        name="put_out",
+    )(graph, relative)
     return graph.reshape(16, BLOCK, BLOCK), relative
 
 

time: 104 us -> 101 us (0.971)
  local copies, waits for them, and re-layouts: 3.41 us -> 0 us
    unnamed x2 -> x0, local copies, waits for them, and re-layouts: 3.41 us -> none
    pallas_call x0 -> x1, Pallas kernels: none -> 3.11 us  [per_device(): pl.pallas_call(copy_kernel, out_shape=(jax.ShapeDtypeStruct(graph.shape,...]
    pallas_call x1, Pallas kernels: 99.7 us -> 97.3 us  [per_device(): pl.pallas_call(kernel, out_shape=(jax.ShapeDtypeStruct((16 * BLOCK, BLOCK...]
where the time goes in v4:
time: 101 us
  Pallas kernels  100 us (99%)
    pallas_call x1, Pallas kernels, per_device(): pl.pallas_call(kernel, out_shape=(jax.ShapeDtypeStruct((16 * BLOCK, BLOCK...  97.3 us
    pallas_call x1, Pallas kernels, per_device(): pl.pallas_call(copy_kernel, out_shape=(jax.ShapeDtypeStruct(graph.shape,...  3.11 us

profile of v4, /device:TPU:1, one launch (start us, length us, event | category | flops | bytes accessed | tf_op | source)
XLA Modules:
  0.0 101.0 jit_solution(842451764040297015)
XLA Ops:
  0.6 97.3 %coarsen.1 = (f32[2048,128]{1,0:T(8,128)}, f32[1,128]{1,0:T(1,128)}) custom-call(bf16[128,128,128]{2,1,0:T(8,128)(2,1)} %blocks.1, s32[2,128]{1,0:T(2,128)} %ids.1, s32[2048,128]{1,0:T(8,128)} %one_hbm.1, s32[1024,128]{1,0:T(8,128)} %two_hbm.1, s32[512,128]{1,0:T(8,128)} %three_hbm.1, s32[1,128]{1,0:T(1,128)} %bitcast.4, s32[1,64]{1,0:T(1,128)} %bitcast.5, ...), custom_call_target="tpu_custom_call" | custom-call | tf_op jit(solution)/shard_map/coarsen/pallas_call | solution.py:383
  97.9 3.1 %put_out.1 = (f32[2048,128]{1,0:T(8,128)}, f32[1,128]{1,0:T(1,128)}) custom-call(f32[2048,128]{1,0:T(8,128)} %get-tuple-element.6.graph, f32[1,128]{1,0:T(1,128)} %get-tuple-element.7.relative), custom_call_target="tpu_custom_call" | custom-call | tf_op jit(solution)/shard_map/put_out/pallas_call | solution.py:437
